TPU v7x, 32 devices: a whole 2x2x4 slice. The times are simulated.
32 devices in a mesh: section: 2 (over x), slab: 16 (over z, y, core).
Axes of the slice: x: 2, y: 2, z: 4, core: 2. Of those that a mesh axis runs over, the one named last changes fastest.
Arguments:
- concentration: float32 [4, 2048, 2048], P('section', 'slab'), may hold values from -3.2 to 3.2
Outputs:
- new_concentration: float32 [4, 2048, 2048], P('section', 'slab')
- energy: float32 [], replicated
All inputs are finite; a program needn't handle non-finite values.
Results may differ from a plain program's by a relative error of at most 0.000098.
Values sent between devices are 32-bit elements; how exact they have to be, the bound alone decides.
A program may use at most 64 MiB of HBM per device.

v0:
```python
import math

import jax
import jax.numpy as jnp
from jax import lax
from jax.sharding import PartitionSpec as P

time_step = 100.0
kappa_grad = 2.0
stabilizer = 8.0
highest = lax.Precision.HIGHEST


def circle(length, first_total, second_total, direction):
    first_index = jnp.arange(first_total, dtype=jnp.int32)
    second_index = jnp.arange(second_total, dtype=jnp.int32)
    turn_index = first_index[:, None] * second_index[None, :] % length
    phase_angle = turn_index.astype(jnp.float32) * (2.0 * math.pi / length)
    return (jnp.cos(phase_angle), direction * jnp.sin(phase_angle))


def contract(pattern, real_part, imag_part, table_cos, table_sin):

    def product_of(operand, matrix):
        return jnp.einsum(pattern, operand, matrix, precision=highest)

    out_real = product_of(real_part, table_cos) - product_of(imag_part, table_sin)
    out_imag = product_of(real_part, table_sin) + product_of(imag_part, table_cos)
    return (out_real, out_imag)


def real_only(pattern, real_part, imag_part, table_cos, table_sin):
    return jnp.einsum(pattern, real_part, table_cos, precision=highest) - jnp.einsum(
        pattern, imag_part, table_sin, precision=highest
    )


def rotate(real_part, imag_part, table_cos, table_sin):
    return (
        real_part * table_cos - imag_part * table_sin,
        real_part * table_sin + imag_part * table_cos,
    )


def wave_square(storage, length, permuted):
    if permuted:
        actual = storage // 128 + length // 128 * (storage % 128)
    else:
        actual = storage
    signed = jnp.where(2 * actual >= length, actual - length, actual)
    phase_angle = signed.astype(jnp.float32) * (2.0 * math.pi / length)
    return phase_angle * phase_angle


def per_device(concentration):
    plane_count, row_count, full_y = concentration.shape
    slab_count = lax.axis_size("slab")
    section_count = lax.axis_size("section")
    full_x = row_count * slab_count
    full_z = plane_count * section_count
    y_block = full_y // slab_count
    y_half = y_block // section_count
    blocks_x = full_x // 128
    blocks_y = full_y // 128
    cell_count = full_x * full_y * full_z
    slab_at = lax.axis_index("slab")
    section_at = lax.axis_index("section")
    squared = concentration * concentration
    bulk_sum = jnp.sum(0.25 * squared * squared - 0.5 * squared)
    cubic_term = squared * concentration - concentration
    shaped_c = concentration.reshape(1, plane_count, row_count, blocks_y, 128)
    shaped_g = cubic_term.reshape(1, plane_count, row_count, blocks_y, 128)
    first_cos, first_sin = circle(blocks_y, blocks_y, blocks_y, -1.0)
    part_real, part_imag = contract("fzxab,aj->fzxjb", shaped_c, shaped_g, first_cos, first_sin)
    field_total = part_real.shape[0]
    twist_cos, twist_sin = circle(full_y, blocks_y, 128, -1.0)
    part_real, part_imag = rotate(part_real, part_imag, twist_cos, twist_sin)
    lane_cos, lane_sin = circle(128, 128, 128, -1.0)
    part_real, part_imag = contract("fzxjb,bk->fxjkz", part_real, part_imag, lane_cos, lane_sin)
    outgoing = jnp.concatenate([part_real, part_imag], 0).reshape(
        2 * field_total, row_count, slab_count, y_block * plane_count
    )
    columns = lax.all_to_all(outgoing, "slab", split_axis=2, concat_axis=1, tiled=True)
    columns = columns.reshape(2 * field_total, blocks_x, 128, y_block * plane_count)
    first_cos, first_sin = circle(blocks_x, blocks_x, blocks_x, -1.0)
    part_real, part_imag = contract(
        "fabm,aj->fmjb", columns[:field_total], columns[field_total:], first_cos, first_sin
    )
    twist_cos, twist_sin = circle(full_x, blocks_x, 128, -1.0)
    part_real, part_imag = rotate(part_real, part_imag, twist_cos, twist_sin)
    part_real, part_imag = contract("fmjb,bk->fmjk", part_real, part_imag, lane_cos, lane_sin)
    spectra_x = jnp.concatenate([part_real, part_imag], 0).reshape(
        2 * field_total, y_block, plane_count, full_x
    )
    depth_cos, depth_sin = circle(full_z, full_z, full_z, -1.0)
    own_cos = lax.dynamic_slice_in_dim(depth_cos, section_at * plane_count, plane_count, 0)
    own_sin = lax.dynamic_slice_in_dim(depth_sin, section_at * plane_count, plane_count, 0)
    term_real, term_imag = contract(
        "fyzk,zq->yfqk", spectra_x[:field_total], spectra_x[field_total:], own_cos, own_sin
    )
    spectral = lax.psum_scatter(
        jnp.concatenate([term_real, term_imag], 1), "section", scatter_dimension=0, tiled=True
    )
    storage_y = slab_at * y_block + section_at * y_half + jnp.arange(y_half, dtype=jnp.int32)
    storage_x = jnp.arange(full_x, dtype=jnp.int32)
    storage_z = jnp.arange(full_z, dtype=jnp.int32)
    wave_sq = (
        wave_square(storage_y, full_y, True)[:, None, None]
        + wave_square(storage_z, full_z, False)[None, :, None]
        + wave_square(storage_x, full_x, True)[None, None, :]
    )
    numerator = 1.0 + time_step * stabilizer * wave_sq
    denominator = numerator + time_step * kappa_grad * wave_sq * wave_sq
    keep_rate = numerator / denominator
    mix_rate = time_step * wave_sq / denominator
    new_real = keep_rate * spectral[:, 0] - mix_rate * spectral[:, 1]
    new_imag = keep_rate * spectral[:, 1] + mix_rate * spectral[:, 0]
    back_cos, back_sin = circle(full_z, full_z, full_z, 1.0)
    part_real, part_imag = contract("yqk,qz->yzk", new_real, new_imag, back_cos, back_sin)
    returning = jnp.stack([part_real, part_imag], 1)
    own_planes = lax.all_to_all(returning, "section", split_axis=2, concat_axis=0, tiled=True)
    grid_real = own_planes[:, 0].reshape(y_block, plane_count, blocks_x, 128)
    grid_imag = own_planes[:, 1].reshape(y_block, plane_count, blocks_x, 128)
    lane_cos, lane_sin = circle(128, 128, 128, 1.0)
    part_real, part_imag = contract("szjk,kb->szjb", grid_real, grid_imag, lane_cos, lane_sin)
    twist_cos, twist_sin = circle(full_x, blocks_x, 128, 1.0)
    part_real, part_imag = rotate(part_real, part_imag, twist_cos, twist_sin)
    first_cos, first_sin = circle(blocks_x, blocks_x, blocks_x, 1.0)
    part_real, part_imag = contract("szjb,ja->absz", part_real, part_imag, first_cos, first_sin)
    leaving = jnp.stack([part_real, part_imag], 0).reshape(2, full_x, 1, y_block * plane_count)
    rows_back = lax.all_to_all(leaving, "slab", split_axis=1, concat_axis=2, tiled=True)
    rows_back = rows_back.reshape(2, row_count, blocks_y, 128, plane_count)
    part_real, part_imag = contract("xjkz,kb->xjbz", rows_back[0], rows_back[1], lane_cos, lane_sin)
    twist_cos, twist_sin = circle(full_y, blocks_y, 128, 1.0)
    part_real, part_imag = rotate(
        part_real, part_imag, twist_cos[:, :, None], twist_sin[:, :, None]
    )
    first_cos, first_sin = circle(blocks_y, blocks_y, blocks_y, 1.0)
    new_field = real_only("xjbz,ja->zxab", part_real, part_imag, first_cos, first_sin)
    new_field = new_field.reshape(plane_count, row_count, full_y) / cell_count
    total_bulk = lax.psum(bulk_sum, ("section", "slab"))
    energy = total_bulk / cell_count
    return (new_field, energy)


def solution(mesh):
    return jax.shard_map(
        per_device,
        mesh=mesh,
        in_specs=(P("section", "slab", None),),
        out_specs=(P("section", "slab", None), P()),
        check_vma=False,
    )
```

profile of v0, /device:TPU:0, one launch (start us, length us, event | category | flops | bytes accessed | tf_op | source)
XLA Modules:
  0.0 700.4 jit_solution(8344704783409716952)
XLA Ops:
  39.9 7.5 %all-to-all-start = ((f32[2,128,16,256]{3,1,0,2:T(8,128)}), f32[2,128,16,256]{3,1,0,2:T(8,128)}, u32[]{:S(2)}, u32[]{:S(2)}) async-start(f32[2,128,16,256]{3,1,0,2:T(8,128)} %copy.129), calls=%async_computation | async-start | bytes 8388608 | tf_op jit(solution)/shard_map/all_to_all | solution.py:83
  48.0 77.0 %all-to-all-done = f32[2,128,16,256]{3,1,0,2:T(8,128)} async-done(((f32[2,128,16,256]{3,1,0,2:T(8,128)}), f32[2,128,16,256]{3,1,0,2:T(8,128)}, u32[]{:S(2)}, u32[]{:S(2)}) %all-to-all-start) | async-done | bytes 4194336 | tf_op jit(solution)/shard_map/all_to_all | solution.py:83
  169.0 8.9 %fusion.194 = f32[4,128,2048]{2,0,1:T(4,128)S(1)} fusion(f32[128,2,2048]{2,1,0:T(2,128)S(1)} %reshape.365, f32[4,4]{1,0:T(4,128)S(1)} %fusion.197, s32[]{:T(128)S(6)} %select_n.234), kind=kOutput, calls=%fused_computation.226 | convolution fusion | flops 25165824 | bytes 6292484 | tf_op jit(solution)/shard_map/fyzk,zq->yfqk/dot_general | solution.py:25
  177.9 9.1 %fusion.190 = f32[4,128,2048]{2,0,1:T(4,128)S(1)} fusion(f32[128,2,2048]{2,1,0:T(2,128)S(1)} %reshape.365, f32[4,4]{1,0:T(4,128)S(1)} %broadcast_multiply_fusion.1, s32[]{:T(128)S(6)} %select_n.234), kind=kOutput, calls=%fused_computation.222 | convolution fusion | flops 25165824 | bytes 6292484 | tf_op jit(solution)/shard_map/fyzk,zq->yfqk/dot_general | solution.py:25
  187.1 9.4 %subtract_bitcast_fusion = f32[128,1,4,2048]{3,2,0,1:T(4,128)S(1)} fusion(f32[4,128,2048]{2,0,1:T(4,128)S(1)} %fusion.194, f32[128,2,2048]{2,1,0:T(2,128)S(1)} %copy-done.1, f32[4,4]{1,0:T(4,128)S(1)} %broadcast_multiply_fusion.1, s32[]{:T(128)S(6)} %select_n.234), kind=kOutput, calls=%fused_computation.10 | convolution fusion | flops 26214400 | bytes 10486788 | tf_op jit(solution)/shard_map/fyzk,zq->yfqk/dot_general | solution.py:25
  196.5 11.2 %add_bitcast_fusion = f32[128,1,4,2048]{3,2,0,1:T(4,128)} fusion(f32[4,128,2048]{2,0,1:T(4,128)S(1)} %fusion.190, f32[128,2,2048]{2,1,0:T(2,128)S(1)} %copy-done.1, f32[4,4]{1,0:T(4,128)S(1)} %fusion.197, s32[]{:T(128)S(6)} %select_n.234), kind=kOutput, calls=%fused_computation.9 | convolution fusion | flops 26214400 | bytes 10486788 | tf_op jit(solution)/shard_map/fyzk,zq->yfqk/dot_general | solution.py:25
  207.7 8.6 %pad_maximum_fusion = f32[128,2,4,2048]{3,2,0,1:T(4,128)} fusion(f32[128,1,4,2048]{3,2,0,1:T(4,128)} %add_bitcast_fusion, f32[128,1,4,2048]{3,2,0,1:T(4,128)S(1)} %subtract_bitcast_fusion), kind=kLoop, calls=%fused_computation | loop fusion | flops 2097152 | bytes 16777216 | tf_op jit(solution)/shard_map/concatenate | solution.py:102
  216.3 10.4 %copy.210 = f32[128,2,4,2048]{3,2,1,0:T(4,128)} copy(f32[128,2,4,2048]{3,2,0,1:T(4,128)} %pad_maximum_fusion) | data formatting | bytes 16777216
  226.6 10.9 %reshape.390 = f32[128,16384]{1,0:T(8,128)} reshape(f32[128,2,4,2048]{3,2,1,0:T(4,128)} %copy.210) | data formatting | bytes 16777216
  237.7 114.4 %reduce-scatter.5.cloned.1.call-done = f32[64,16384]{1,0:T(8,128)} async-done(((f32[128,16384]{1,0:T(8,128)}), f32[64,16384]{1,0:T(8,128)}) %reduce-scatter.5.cloned.1.call-update) | async-done | bytes 4194320
  352.1 6.0 reshape.391
  371.0 6.6 fusion.1
  377.7 6.8 fusion
  391.0 5.6 all-to-all-start.1
  396.6 47.4 %all-to-all-done.1 = f32[64,2,4,2048]{3,0,1,2:T(8,128)} async-done(((f32[64,2,4,2048]{3,0,1,2:T(8,128)}), f32[64,2,4,2048]{3,0,1,2:T(8,128)}, u32[]{:S(2)}, u32[]{:S(2)}) %all-to-all-start.1) | async-done | bytes 4194336 | tf_op jit(solution)/shard_map/all_to_all | solution.py:121
  464.1 5.4 convolution_subtract_fusion.2
  469.5 5.4 multiply_subtract_fusion.1
  489.1 6.0 copy.164
  495.2 5.8 add_bitcast_fusion.1
  506.3 8.1 %pad_maximum_fusion.3 = f32[2,2048,1,256]{3,2,0,1:T(1,128)} fusion(f32[1,2048,1,256]{3,2,0,1:T(1,128)} %copy.165, f32[1,2048,1,256]{3,2,0,1:T(1,128)} %copy.164), kind=kLoop, calls=%fused_computation.7 | loop fusion | flops 1048576 | bytes 8388608 | tf_op jit(solution)/shard_map/stack | solution.py:130
  514.3 5.7 all-to-all-start.2
  520.0 113.2 %psum.7 = f32[]{:T(128)} all-reduce(f32[]{:T(128)} %get-tuple-element.22), channel_id=1, replica_groups=mesh['section'=2,'slab'=16] {'section','slab'}, use_global_device_ids=true, to_apply=%region_2.3 | all-reduce | flops 1 | bytes 8 | tf_op jit(solution)/shard_map/psum | solution.py:141
  633.9 8.0 %copy.212 = f32[2,2048,1,256]{3,0,2,1:T(2,128)} copy(f32[2,2048,1,256]{3,2,0,1:T(1,128)} %all-to-all-done.2) | data formatting | bytes 8388608
  641.9 5.3 copy.209
  (86 shorter events, 180.9 us)
Async XLA Ops:
  10.4 2.0 copy-start.6
  39.9 85.0 %all-to-all-start = ((f32[2,128,16,256]{3,1,0,2:T(8,128)}), f32[2,128,16,256]{3,1,0,2:T(8,128)}, u32[]{:S(2)}, u32[]{:S(2)}) async-start(f32[2,128,16,256]{3,1,0,2:T(8,128)} %copy.129), calls=%async_computation | async-start | bytes 8388608 | tf_op jit(solution)/shard_map/all_to_all | solution.py:83
  47.4 304.7 %reduce-scatter.5.cloned.1.call-start = ((), (), s32[]{:S(2)}) async-start(), calls=%async_computation.4 | async-start | bytes 12582912
  177.9 9.2 %copy-start.1 = (f32[128,2,2048]{2,1,0:T(2,128)S(1)}, f32[128,2,2048]{2,1,0:T(2,128)}, u32[]{:S(2)}) copy-start(f32[128,2,2048]{2,1,0:T(2,128)} %reshape.366) | copy-start | bytes 6291460
  366.4 4.6 copy-start.2
  391.0 53.1 %all-to-all-start.1 = ((f32[64,2,4,2048]{3,0,1,2:T(8,128)}), f32[64,2,4,2048]{3,0,1,2:T(8,128)}, u32[]{:S(2)}, u32[]{:S(2)}) async-start(f32[64,2,4,2048]{3,0,1,2:T(8,128)} %copy.147), calls=%async_computation.1 | async-start | bytes 8388608 | tf_op jit(solution)/shard_map/all_to_all | solution.py:121
  462.8 1.3 copy-start
  464.1 5.4 copy-start.5
  514.3 119.6 %all-to-all-start.2 = ((f32[2,2048,1,256]{3,2,0,1:T(1,128)}), f32[2,2048,1,256]{3,2,0,1:T(1,128)}, u32[]{:S(2)}, u32[]{:S(2)}) async-start(f32[2,2048,1,256]{3,2,0,1:T(1,128)} %pad_maximum_fusion.3), calls=%async_computation.2 | async-start | bytes 8388608 | tf_op jit(solution)/shard_map/all_to_all | solution.py:131
  662.6 3.9 copy-start.3
  674.6 5.0 copy-start.4
Sparse Core Ops, SparseCore 0:
  237.7 114.3 reduce-scatter.4
where the time goes:
time: 711 us; the launch traced here: 700 us
  waiting for transfers between devices  239 us (34%)
  matrix products  167 us (23%)
  local copies, waits for them, and re-layouts  119 us (17%)
  blocking collectives  113 us (16%)
  other arithmetic  25.7 us (4%)
  starting transfers between devices  19 us (3%)
  between operations  16.7 us (2%)
    dot_general x36, matrix products, product_of(): return jnp.einsum(pattern, operand, matrix, precision=highest)  158 us
    unnamed x2, waiting for transfers between devices  114 us
    psum x1, blocking collectives, per_device(): total_bulk = lax.psum(bulk_sum, ('section', 'slab'))  113 us
    all_to_all x1, waiting for transfers between devices, per_device(): lax.all_to_all(outgoing, 'slab', split_axis=2, concat_axis=1, tiled=True)  77 us
    all_to_all x1, waiting for transfers between devices, per_device(): lax.all_to_all(returning, 'section', split_axis=2, concat_axis=0, tiled=T...  47.4 us
    unnamed x21, local copies, waits for them, and re-layouts  41.5 us
  transfers between devices with their start and end apart: 4, of which 3 were waited for; matrix products, arithmetic and copies ran while one was open for 0% of the time, Pallas kernels for 0%

commit v1 on v0

--- a/solution.py
+++ b/solution.py
@@ -1,8 +1,12 @@
+import functools
 import math
 
 import jax
 import jax.numpy as jnp
+import numpy as np
 from jax import lax
+from jax.experimental import pallas as pl
+from jax.experimental.pallas import tpu as pltpu
 from jax.sharding import PartitionSpec as P
 
 time_step = 100.0
@@ -52,7 +56,7 @@
     return phase_angle * phase_angle
 
 
-def per_device(concentration):
+def plain_step(concentration):
     plane_count, row_count, full_y = concentration.shape
     slab_count = lax.axis_size("slab")
     section_count = lax.axis_size("section")
@@ -143,6 +147,385 @@
     return (new_field, energy)
 
 
+lanes = 128
+row_group = 32
+vmem_limit = 60 * 1024 * 1024
+
+
+def split(values):
+    high = values.astype(jnp.bfloat16)
+    low = (values - high.astype(jnp.float32)).astype(jnp.bfloat16)
+    return high, low
+
+
+def triple(left_parts, right_parts, dims):
+    def product(left, right):
+        return lax.dot_general(left, right, (dims, ((), ())), preferred_element_type=jnp.float32)
+
+    left_high, left_low = left_parts
+    right_high, right_low = right_parts
+    return (
+        product(left_high, right_high)
+        + product(left_low, right_high)
+        + product(left_high, right_low)
+    )
+
+
+def y_tables(full_y, devices, parity):
+    half = full_y // 2
+    per_part = half // 2 // devices
+    slot = np.arange(half)
+    device, inner = slot // (2 * per_part), slot % (2 * per_part)
+    part, local = inner // per_part, inner % per_part
+    wave = parity + 2 * (device * per_part + local)
+    position = np.arange(half)
+    turns = wave[:, None] * position[None, :] % full_y
+    phase = turns * (2.0 * math.pi / full_y)
+    coarse = phase[::row_group]
+    offset = wave[:row_group] - wave[0]
+    fine = (offset[:, None] * position[None, :] % full_y) * (2.0 * math.pi / full_y)
+    fine = fine + part[:row_group, None] * (0.5 * math.pi)
+    return [
+        table.astype(np.float32)
+        for table in (np.cos(coarse), np.sin(coarse), np.cos(fine), np.sin(fine))
+    ]
+
+
+def y_block(refs, block, groups, parity):
+    coarse_cos, coarse_sin, fine_cos, fine_sin = refs
+    cos_fine, sin_fine = fine_cos[...], fine_sin[...]
+    width = cos_fine.shape[1]
+    pieces = []
+    for group in range(block * groups, (block + 1) * groups):
+        piece = coarse_cos[group : group + 1, :] * cos_fine - coarse_sin[group : group + 1, :] * sin_fine
+        if parity == 0 and group == 0:
+            row = lax.broadcasted_iota(jnp.int32, piece.shape, 0)
+            column = lax.broadcasted_iota(jnp.int32, piece.shape, 1)
+            sign = 1.0 - 2.0 * (column % 2).astype(jnp.float32)
+            piece = jnp.where(row == row_group // 2, sign, piece)
+        pieces.append(piece)
+    return jnp.concatenate(pieces, 0)
+
+
+def forward_kernel(parity, conc_ref, ta, tb, tc, td, out_ref, high_ref, low_ref):
+    planes, rows, full_y = conc_ref.shape
+    half = full_y // 2
+    for plane in range(planes):
+        first = conc_ref[plane, :, :half]
+        second = conc_ref[plane, :, half:]
+        first_g = first * first * first - first
+        second_g = second * second * second - second
+        for field, (left, right) in enumerate(((first, second), (first_g, second_g))):
+            mixed = left + right if parity == 0 else left - right
+            high, low = split(mixed)
+            at = (plane * 2 + field) * rows
+            high_ref[at : at + rows, :] = high
+            low_ref[at : at + rows, :] = low
+    groups = 8
+    for block in range(half // (groups * row_group)):
+        table = y_block((ta, tb, tc, td), block, groups, parity)
+        result = triple(split(table), (high_ref[...], low_ref[...]), ((1,), (1,)))
+        out_ref[block * groups : (block + 1) * groups] = result.reshape(groups, row_group, -1)
+
+
+def backward_part(parity, in_ref, tables):
+    devices, inner, columns = in_ref.shape
+    groups = 8
+    total = None
+    for block in range(devices // groups):
+        rows = in_ref[block * groups : (block + 1) * groups].reshape(groups * inner, columns)
+        table = y_block(tables, block, groups, parity)
+        term = triple(split(rows.T), split(table), ((1,), (0,)))
+        total = term if total is None else total + term
+    return total
+
+
+def backward_even_kernel(in_ref, ta, tb, tc, td, out_ref):
+    out_ref[...] = backward_part(0, in_ref, (ta, tb, tc, td))
+
+
+def backward_odd_kernel(in_ref, even_ref, ta, tb, tc, td, out_ref):
+    planes, rows, full_y = out_ref.shape
+    half = full_y // 2
+    odd = backward_part(1, in_ref, (ta, tb, tc, td))
+    for plane in range(planes):
+        even_rows = even_ref[plane * rows : (plane + 1) * rows, :]
+        odd_rows = odd[plane * rows : (plane + 1) * rows, :]
+        out_ref[plane, :, :half] = even_rows + odd_rows
+        out_ref[plane, :, half:] = even_rows - odd_rows
+
+
+def times_unit(real, imag, quarter_turns):
+    turns = quarter_turns % 4
+    if turns == 0:
+        return real, imag
+    if turns == 1:
+        return -imag, real
+    if turns == 2:
+        return -real, -imag
+    return imag, -real
+
+
+def unit_sum(parts, power, direction):
+    total_real, total_imag = parts[0]
+    for index in range(1, len(parts)):
+        real, imag = times_unit(*parts[index], direction * power * index)
+        total_real = total_real + real
+        total_imag = total_imag + imag
+    return total_real, total_imag
+
+
+def middle_kernel(
+    has_extra, sections, in_ref, aux_ref, wx_ref, tw_cos, tw_sin, high_ref, low_ref, out_ref,
+    spec_ref, fil_ref, back_ref,
+):
+    devices, inner, columns = in_ref.shape
+    kk = inner // 2
+    slabs = devices // sections
+    zf_local = columns // lanes
+    planes = zf_local // 2
+    full_z = planes * sections
+    quarter = slabs // 4
+    width = quarter * lanes
+    padded = spec_ref.shape[3]
+    special = aux_ref[2, 0:8, 0:1] if has_extra else None
+
+    def gather(section, a, part, row, zf):
+        pieces = [
+            in_ref[
+                section * slabs + a * quarter + step,
+                part * kk + row : part * kk + row + 8,
+                zf * lanes : (zf + 1) * lanes,
+            ]
+            for step in range(quarter)
+        ]
+        return jnp.concatenate(pieces, 1)
+
+    for section in range(sections):
+        for zf in range(zf_local):
+            at = section * zf_local + zf
+            for row in range(0, padded, 8):
+                source = 0 if row >= kk else row
+                parts = []
+                for a in range(4):
+                    imag = gather(section, a, 1, source, zf)
+                    if row >= kk:
+                        real, imag = imag * special, jnp.zeros_like(imag)
+                    else:
+                        real = gather(section, a, 0, source, zf)
+                        if has_extra and row == 0:
+                            imag = imag * (1.0 - special)
+                    parts.append((real, imag))
+                for j in range(4):
+                    real, imag = unit_sum(parts, j, -1)
+                    if j:
+                        cos, sin = tw_cos[j : j + 1, :], tw_sin[j : j + 1, :]
+                        real, imag = real * cos + imag * sin, imag * cos - real * sin
+                    spec_ref[j, 0, at, row : row + 8, :] = real
+                    spec_ref[j, 1, at, row : row + 8, :] = imag
+
+    weights = (high_ref[...], low_ref[...])
+    total_zf = sections * zf_local
+    for j in range(4):
+        rows = spec_ref[j].reshape(2 * total_zf * padded, width)
+        raw = triple(split(rows), weights, ((1,), (0,)))
+        raw = raw.reshape(2, total_zf, padded, 2 * width)
+        for row in range(0, padded, 8):
+            fields = []
+            for field in range(2):
+                per_z = []
+                for z in range(full_z):
+                    at = z * 2 + field
+                    re_part = raw[0, at, row : row + 8]
+                    im_part = raw[1, at, row : row + 8]
+                    per_z.append(
+                        (
+                            re_part[:, :width] + im_part[:, width:],
+                            im_part[:, :width] - re_part[:, width:],
+                        )
+                    )
+                fields.append(per_z)
+            plane_sq = aux_ref[0, row : row + 8, 0:1] + wx_ref[j : j + 1, :]
+            weight = aux_ref[1, row : row + 8, 0:1]
+            updated = []
+            for q in range(full_z):
+                c_real, c_imag = unit_sum(fields[0], q, -1)
+                g_real, g_imag = unit_sum(fields[1], q, -1)
+                signed = q - full_z if 2 * q >= full_z else q
+                wave_sq = plane_sq + (2.0 * math.pi * signed / full_z) ** 2
+                numerator = 1.0 + time_step * stabilizer * wave_sq
+                denominator = numerator + time_step * kappa_grad * wave_sq * wave_sq
+                inverse = weight / denominator
+                keep = numerator * inverse
+                mix = time_step * wave_sq * inverse
+                updated.append((keep * c_real - mix * g_real, keep * c_imag - mix * g_imag))
+            for z in range(full_z):
+                real, imag = unit_sum(updated, z, 1)
+                fil_ref[0, z, row : row + 8, :] = real
+                fil_ref[1, z, row : row + 8, :] = imag
+        rows = fil_ref[...].reshape(2 * full_z * padded, width)
+        raw = triple(split(rows), weights, ((1,), (0,)))
+        raw = raw.reshape(2, full_z, padded, 2 * width)
+        real = raw[0, :, :, :width] - raw[1, :, :, width:]
+        imag = raw[0, :, :, width:] + raw[1, :, :, :width]
+        cos, sin = tw_cos[j : j + 1, :], tw_sin[j : j + 1, :]
+        back_ref[j, 0] = real * cos - imag * sin
+        back_ref[j, 1] = imag * cos + real * sin
+
+    for z in range(full_z):
+        section, plane = z // planes, z % planes
+        for row in range(0, kk, 8):
+            parts = [
+                (back_ref[j, 0, z, row : row + 8, :], back_ref[j, 1, z, row : row + 8, :])
+                for j in range(4)
+            ]
+            extra = None
+            if has_extra and row == 0:
+                extra = [
+                    (back_ref[j, 0, z, kk : kk + 8, :], back_ref[j, 1, z, kk : kk + 8, :])
+                    for j in range(4)
+                ]
+            for a in range(4):
+                real, imag = unit_sum(parts, a, 1)
+                if extra is not None:
+                    extra_real, _ = unit_sum(extra, a, 1)
+                    imag = imag * (1.0 - special) + extra_real * special
+                for step in range(quarter):
+                    target = section * slabs + a * quarter + step
+                    piece = slice(step * lanes, (step + 1) * lanes)
+                    column = slice(plane * lanes, (plane + 1) * lanes)
+                    out_ref[target, row : row + 8, column] = real[:, piece]
+                    out_ref[target, kk + row : kk + row + 8, column] = imag[:, piece]
+
+
+def kernel_call(body, out_shape, scratch, flops, moved, *operands):
+    return pl.pallas_call(
+        body,
+        out_shape=jax.ShapeDtypeStruct(out_shape, jnp.float32),
+        in_specs=[pl.BlockSpec(memory_space=pltpu.VMEM)] * len(operands),
+        out_specs=pl.BlockSpec(memory_space=pltpu.VMEM),
+        scratch_shapes=scratch,
+        compiler_params=pltpu.CompilerParams(vmem_limit_bytes=vmem_limit),
+        cost_estimate=pl.CostEstimate(flops=flops, bytes_accessed=moved, transcendentals=0),
+    )(*operands)
+
+
+def signed_square(index, length):
+    signed = jnp.where(2 * index >= length, index - length, index)
+    angle = signed.astype(jnp.float32) * (2.0 * math.pi / length)
+    return angle * angle
+
+
+def kernel_step(concentration):
+    planes, rows, full_y = concentration.shape
+    slabs = lax.axis_size("slab")
+    sections = lax.axis_size("section")
+    devices = slabs * sections
+    full_x = rows * slabs
+    full_z = planes * sections
+    cells = full_x * full_y * full_z
+    half = full_y // 2
+    kk = half // 2 // devices
+    width = full_x // 4
+    me = lax.axis_index("section") * slabs + lax.axis_index("slab")
+    axes = ("section", "slab")
+    base = np.arange(width)
+    turn = (base[:, None] * base[None, :] % width) * (2.0 * math.pi / width)
+    dft = np.concatenate([np.cos(turn), np.sin(turn)], 1).astype(np.float32)
+    dft_high = dft.astype(jnp.bfloat16)
+    dft_low = (dft - dft_high.astype(np.float32)).astype(jnp.bfloat16)
+    twist = np.arange(4)[:, None] * base[None, :] * (2.0 * math.pi / full_x)
+    twist_cos, twist_sin = np.cos(twist).astype(np.float32), np.sin(twist).astype(np.float32)
+    kx = np.arange(4)[:, None] + 4 * base[None, :]
+    kx = np.where(2 * kx >= full_x, kx - full_x, kx) * (2.0 * math.pi / full_x)
+    wave_x = (kx * kx).astype(np.float32)
+    tables = [y_tables(full_y, devices, parity) for parity in range(2)]
+    columns = planes * 2 * rows
+    flops = 6 * half * half * columns
+    arrived = []
+    for parity in range(2):
+        sent = kernel_call(
+            functools.partial(forward_kernel, parity),
+            (devices, 2 * kk, columns),
+            [pltpu.VMEM((columns, half), jnp.bfloat16)] * 2,
+            flops,
+            4 * concentration.size + 4 * half * columns,
+            concentration,
+            *tables[parity],
+        )
+        arrived.append(lax.all_to_all(sent, axes, split_axis=0, concat_axis=0, tiled=True))
+    returned = []
+    for parity in range(2):
+        has_extra = parity == 0
+        padded = kk + 8 if has_extra else kk
+        row = jnp.arange(padded, dtype=jnp.int32)
+        wave = parity + 2 * (me * kk + row)
+        extra_row = row >= kk
+        if has_extra:
+            wave = jnp.where(extra_row, half, wave)
+        first = (wave == 0) | extra_row
+        weight = jnp.where(first, 1.0 / cells, 2.0 / cells)
+        flag = jnp.where((row == 0) & (me == 0), 1.0, 0.0)
+        aux = jnp.stack([signed_square(wave, full_y), weight, flag]).astype(jnp.float32)
+        aux = jnp.broadcast_to(aux[:, :, None], (3, padded, lanes))
+        sent = kernel_call(
+            functools.partial(middle_kernel, has_extra, sections),
+            (devices, 2 * kk, planes * rows),
+            [
+                pltpu.VMEM((4, 2, 2 * full_z, padded, width), jnp.float32),
+                pltpu.VMEM((2, full_z, padded, width), jnp.float32),
+                pltpu.VMEM((4, 2, full_z, padded, width), jnp.float32),
+            ],
+            6 * 24 * full_z * padded * width * 2 * width,
+            4 * half * columns,
+            arrived[parity],
+            aux,
+            wave_x,
+            twist_cos,
+            twist_sin,
+            dft_high,
+            dft_low,
+        )
+        returned.append(lax.all_to_all(sent, axes, split_axis=0, concat_axis=0, tiled=True))
+    even = kernel_call(
+        backward_even_kernel,
+        (planes * rows, half),
+        [],
+        flops // 2,
+        8 * half * columns,
+        returned[0],
+        *tables[0],
+    )
+    new_field = kernel_call(
+        backward_odd_kernel,
+        concentration.shape,
+        [],
+        flops // 2,
+        8 * half * columns,
+        returned[1],
+        even,
+        *tables[1],
+    )
+    squared = concentration * concentration
+    bulk_sum = jnp.sum(0.25 * squared * squared - 0.5 * squared)
+    energy = lax.psum(bulk_sum, axes) / cells
+    return (new_field, energy)
+
+
+def per_device(concentration):
+    planes, rows, full_y = concentration.shape
+    devices = lax.axis_size("slab") * lax.axis_size("section")
+    share = full_y // 4 // devices
+    fits = (
+        rows == lanes
+        and planes * lax.axis_size("section") == 4
+        and 2 * share == row_group
+        and devices % 8 == 0
+        and lax.axis_size("slab") % 4 == 0
+    )
+    return kernel_step(concentration) if fits else plain_step(concentration)
+
+
 def solution(mesh):
     return jax.shard_map(
         per_device,

time: 711 us -> 210 us (0.30); the launches traced: 700 us -> 210 us
  matrix products: 167 us -> 0 us
  waiting for transfers between devices: 239 us -> 96.6 us
  local copies, waits for them, and re-layouts: 119 us -> 2.72 us
  blocking collectives: 113 us -> 45.1 us
  Pallas kernels: 0 us -> 45 us
  other arithmetic: 25.7 us -> 1.21 us
  between operations: 16.7 us -> 2.51 us
    dot_general x38 -> x0, matrix products: 167 us -> none  [the longest x36 158 us: product_of(): return jnp.einsum(pattern, operand, matrix, precision=highest)]
    unnamed x2 -> x0, waiting for transfers between devices: 114 us -> none
    psum x1, blocking collectives: 113 us -> 45.1 us  [kernel_step(): energy = lax.psum(bulk_sum, axes) / cells]
    pallas_call x0 -> x6, Pallas kernels: none -> 45 us  [kernel_call(): pl.pallas_call(body, out_shape=jax.ShapeDtypeStruct(out_shape, jnp.float3...]
    unnamed x21 -> x8, local copies, waits for them, and re-layouts: 41.5 us -> 1.35 us
    another operation x9 -> x0, local copies, waits for them, and re-layouts: 28.2 us -> none  [the longest x4 14.1 us: per_device(): jnp.stack([part_real, part_imag], 0)]
    all_to_all x3 -> x4, waiting for transfers between devices: 124 us -> 96.6 us  [kernel_step(): lax.all_to_all(sent, axes, split_axis=0, concat_axis=0, tiled=True)]
    all_to_all x3 -> x0, local copies, waits for them, and re-layouts: 12.4 us -> none  [the longest x1 5.3 us: per_device(): lax.all_to_all(leaving, 'slab', split_axis=1, concat_axis=2, tiled=True)]
  transfers between devices with their start and end apart: 4 -> 4, of which waited for: 3 -> 3; matrix products, arithmetic and copies ran while one was open for 0% -> 1% of each run, Pallas kernels for 0% -> 16%
where the time goes in v1:
time: 210 us
  waiting for transfers between devices  96.6 us (46%)
  blocking collectives  45.1 us (21%)
  Pallas kernels  45 us (21%)
  starting transfers between devices  16.5 us (8%)
  local copies, waits for them, and re-layouts  2.72 us (1%)
  between operations  2.51 us (1%)
    all_to_all x4, waiting for transfers between devices, kernel_step(): lax.all_to_all(sent, axes, split_axis=0, concat_axis=0, tiled=True)  96.6 us
    psum x1, blocking collectives, kernel_step(): energy = lax.psum(bulk_sum, axes) / cells  45.1 us
    pallas_call x6, Pallas kernels, kernel_call(): pl.pallas_call(body, out_shape=jax.ShapeDtypeStruct(out_shape, jnp.float3...  45 us
    all_to_all x4, starting transfers between devices, kernel_step(): lax.all_to_all(sent, axes, split_axis=0, concat_axis=0, tiled=True)  16.5 us
  transfers between devices with their start and end apart: 4, of which 3 were waited for; matrix products, arithmetic and copies ran while one was open for 1% of the time, Pallas kernels for 16%

profile of v1, /device:TPU:0, one launch (start us, length us, event | category | flops | bytes accessed | tf_op | source)
XLA Modules:
  0.0 209.7 jit_solution(1372445717697540948)
XLA Ops:
  0.6 6.8 %shard_map.151 = f32[32,32,512]{2,1,0:T(8,128)} custom-call(f32[2,128,2048]{2,1,0:T(8,128)} %conc_ref.3, f32[32,1024]{1,0:T(8,128)} %constant.71.clone.ta, f32[32,1024]{1,0:T(8,128)} %constant.72.clone.tb, f32[32,1024]{1,0:T(8,128)} %constant.73.clone.tc, f32[32,1024]{1,0:T(8,128)} %constant.74.clone.td), custom_call_target="tpu_custom_call" | custom-call | flops 3221225472 | bytes 4194304 | tf_op jit(solution)/shard_map/pallas_call | solution.py:402
  7.5 7.3 %all-to-all-start.2 = ((f32[32,32,512]{2,1,0:T(8,128)}), f32[32,32,512]{2,1,0:T(8,128)S(1)}, u32[]{:S(2)}, u32[]{:S(2)}) async-start(f32[32,32,512]{2,1,0:T(8,128)} %shard_map.151), calls=%async_computation.2 | async-start | bytes 4194304 | tf_op jit(solution)/shard_map/all_to_all | solution.py:456
  14.8 6.8 %shard_map.149 = f32[32,32,512]{2,1,0:T(8,128)} custom-call(f32[2,128,2048]{2,1,0:T(8,128)} %conc_ref.3, f32[32,1024]{1,0:T(8,128)} %constant.75.clone.ta, f32[32,1024]{1,0:T(8,128)} %constant.76.clone.tb, f32[32,1024]{1,0:T(8,128)} %constant.73.clone.tc, f32[32,1024]{1,0:T(8,128)} %constant.74.clone.td), custom_call_target="tpu_custom_call" | custom-call | flops 3221225472 | bytes 4194304 | tf_op jit(solution)/shard_map/pallas_call | solution.py:402
  21.6 43.2 %all-to-all-done.2.in_ref = f32[32,32,512]{2,1,0:T(8,128)S(1)} async-done(((f32[32,32,512]{2,1,0:T(8,128)}), f32[32,32,512]{2,1,0:T(8,128)S(1)}, u32[]{:S(2)}, u32[]{:S(2)}) %all-to-all-start.2) | async-done | bytes 2097184 | tf_op jit(solution)/shard_map/all_to_all | solution.py:456
  64.9 0.0 copy-start.2
  64.9 1.3 copy-done.2
  66.2 2.9 %all-to-all-start = ((f32[32,32,512]{2,1,0:T(8,128)}), f32[32,32,512]{2,1,0:T(8,128)S(1)}, u32[]{:S(2)}, u32[]{:S(2)}) async-start(f32[32,32,512]{2,1,0:T(8,128)} %shard_map.149), calls=%async_computation | async-start | bytes 4194304 | tf_op jit(solution)/shard_map/all_to_all | solution.py:456
  69.2 0.7 broadcast_in_dim.54.aux_ref
  69.9 12.2 %shard_map.152 = f32[32,32,256]{2,1,0:T(8,128)} custom-call(f32[32,32,512]{2,1,0:T(8,128)} %copy-done.2, f32[3,24,128]{2,1,0:T(8,128)} %broadcast_in_dim.54.aux_ref, f32[4,512]{1,0:T(4,128)} %constant.77.clone.wx_ref, f32[4,512]{1,0:T(4,128)} %constant.78.clone.tw_cos, f32[4,512]{1,0:T(4,128)} %constant.79.clone.tw_sin, ...), custom_call_target="tpu_custom_call" | custom-call | flops 7247757312 | bytes 2097152 | tf_op jit(solution)/shard_map/pallas_call | solution.py:402
  82.1 36.9 %all-to-all-done.in_ref = f32[32,32,512]{2,1,0:T(8,128)S(1)} async-done(((f32[32,32,512]{2,1,0:T(8,128)}), f32[32,32,512]{2,1,0:T(8,128)S(1)}, u32[]{:S(2)}, u32[]{:S(2)}) %all-to-all-start) | async-done | bytes 2097184 | tf_op jit(solution)/shard_map/all_to_all | solution.py:456
  119.1 0.0 copy-start.1
  119.1 2.9 %all-to-all-start.3 = ((f32[32,32,256]{2,1,0:T(8,128)}), f32[32,32,256]{2,1,0:T(8,128)S(1)}, u32[]{:S(2)}, u32[]{:S(2)}) async-start(f32[32,32,256]{2,1,0:T(8,128)} %shard_map.152), calls=%async_computation.3 | async-start | bytes 2097152 | tf_op jit(solution)/shard_map/all_to_all | solution.py:489
  122.0 0.7 broadcast_in_dim.48.aux_ref
  122.7 0.0 copy-done.1
  122.7 9.8 %shard_map.150 = f32[32,32,256]{2,1,0:T(8,128)} custom-call(f32[32,32,512]{2,1,0:T(8,128)} %copy-done.1, f32[3,16,128]{2,1,0:T(8,128)} %broadcast_in_dim.48.aux_ref, f32[4,512]{1,0:T(4,128)} %constant.77.clone.wx_ref, f32[4,512]{1,0:T(4,128)} %constant.78.clone.tw_cos, f32[4,512]{1,0:T(4,128)} %constant.79.clone.tw_sin, ...), custom_call_target="tpu_custom_call" | custom-call | flops 4831838208 | bytes 2097152 | tf_op jit(solution)/shard_map/pallas_call | solution.py:402
  132.5 16.4 %all-to-all-done.3.in_ref = f32[32,32,256]{2,1,0:T(8,128)S(1)} async-done(((f32[32,32,256]{2,1,0:T(8,128)}), f32[32,32,256]{2,1,0:T(8,128)S(1)}, u32[]{:S(2)}, u32[]{:S(2)}) %all-to-all-start.3) | async-done | bytes 1048608 | tf_op jit(solution)/shard_map/all_to_all | solution.py:489
  148.9 3.4 %all-to-all-start.1 = ((f32[32,32,256]{2,1,0:T(8,128)}), f32[32,32,256]{2,1,0:T(8,128)}, u32[]{:S(2)}, u32[]{:S(2)}) async-start(f32[32,32,256]{2,1,0:T(8,128)} %shard_map.150), calls=%async_computation.1 | async-start | bytes 2097152 | tf_op jit(solution)/shard_map/all_to_all | solution.py:489
  152.3 0.0 copy-done
  152.3 1.1 fusion.1
  153.4 0.0 copy-done.3
  153.4 45.1 %psum.7 = f32[]{:T(128)} all-reduce(f32[]{:T(128)} %fusion.1), channel_id=1, replica_groups=mesh['section'=2,'slab'=16] {'section','slab'}, use_global_device_ids=true, to_apply=%region_1.2 | all-reduce | flops 1 | bytes 8 | tf_op jit(solution)/shard_map/psum | solution.py:511
  199.2 4.4 %shard_map.153.even_ref = f32[256,1024]{1,0:T(8,128)} custom-call(f32[32,32,256]{2,1,0:T(8,128)} %copy-done.3, f32[32,1024]{1,0:T(8,128)} %constant.71.clone.ta, f32[32,1024]{1,0:T(8,128)} %constant.72.clone.tb, f32[32,1024]{1,0:T(8,128)} %constant.73.clone.tc, f32[32,1024]{1,0:T(8,128)} %constant.74.clone.td), custom_call_target="tpu_custom_call" | custom-call | flops 1610612736 | bytes 4194304 | tf_op jit(solution)/shard_map/pallas_call | solution.py:402
  203.6 0.0 all-to-all-done.1.in_ref
  203.6 5.0 %shard_map.154 = f32[2,128,2048]{2,1,0:T(8,128)} custom-call(f32[32,32,256]{2,1,0:T(8,128)} %all-to-all-done.1.in_ref, f32[256,1024]{1,0:T(8,128)} %shard_map.153.even_ref, f32[32,1024]{1,0:T(8,128)} %constant.75.clone.ta, f32[32,1024]{1,0:T(8,128)} %constant.76.clone.tb, f32[32,1024]{1,0:T(8,128)} %constant.73.clone.tc, f32[32,1024]{1,0:T(8,128)} %constant.74.clone.td), custom_call_target="tpu_custom_call" | custom-call | flops 1610612736 | bytes 4194304 | tf_op jit(solution)/shard_map/pallas_call | solution.py:402
  (8 shorter events, 0.1 us)
Async XLA Ops:
  7.5 57.4 %all-to-all-start.2 = ((f32[32,32,512]{2,1,0:T(8,128)}), f32[32,32,512]{2,1,0:T(8,128)S(1)}, u32[]{:S(2)}, u32[]{:S(2)}) async-start(f32[32,32,512]{2,1,0:T(8,128)} %shard_map.151), calls=%async_computation.2 | async-start | bytes 4194304 | tf_op jit(solution)/shard_map/all_to_all | solution.py:456
  64.9 1.3 copy-start.2
  66.2 52.9 %all-to-all-start = ((f32[32,32,512]{2,1,0:T(8,128)}), f32[32,32,512]{2,1,0:T(8,128)S(1)}, u32[]{:S(2)}, u32[]{:S(2)}) async-start(f32[32,32,512]{2,1,0:T(8,128)} %shard_map.149), calls=%async_computation | async-start | bytes 4194304 | tf_op jit(solution)/shard_map/all_to_all | solution.py:456
  119.1 3.6 %copy-start.1 = (f32[32,32,512]{2,1,0:T(8,128)}, f32[32,32,512]{2,1,0:T(8,128)S(1)}, u32[]{:S(2)}) copy-start(f32[32,32,512]{2,1,0:T(8,128)S(1)} %all-to-all-done.in_ref) | copy-start | bytes 6291460
  119.1 29.8 %all-to-all-start.3 = ((f32[32,32,256]{2,1,0:T(8,128)}), f32[32,32,256]{2,1,0:T(8,128)S(1)}, u32[]{:S(2)}, u32[]{:S(2)}) async-start(f32[32,32,256]{2,1,0:T(8,128)} %shard_map.152), calls=%async_computation.3 | async-start | bytes 2097152 | tf_op jit(solution)/shard_map/all_to_all | solution.py:489
  132.5 19.8 %copy-start = (f32[2,128,2048]{2,1,0:T(8,128)S(1)}, f32[2,128,2048]{2,1,0:T(8,128)}, u32[]{:S(2)}) copy-start(f32[2,128,2048]{2,1,0:T(8,128)} %conc_ref.3) | copy-start | bytes 6291460
  148.9 4.5 %copy-start.3 = (f32[32,32,256]{2,1,0:T(8,128)}, f32[32,32,256]{2,1,0:T(8,128)S(1)}, u32[]{:S(2)}) copy-start(f32[32,32,256]{2,1,0:T(8,128)S(1)} %all-to-all-done.3.in_ref) | copy-start | bytes 3145732
  148.9 54.7 %all-to-all-start.1 = ((f32[32,32,256]{2,1,0:T(8,128)}), f32[32,32,256]{2,1,0:T(8,128)}, u32[]{:S(2)}, u32[]{:S(2)}) async-start(f32[32,32,256]{2,1,0:T(8,128)} %shard_map.150), calls=%async_computation.1 | async-start | bytes 2097152 | tf_op jit(solution)/shard_map/all_to_all | solution.py:489

commit v2 on v1

--- a/solution.py
+++ b/solution.py
@@ -233,9 +233,15 @@
     groups = 8
     total = None
     for block in range(devices // groups):
-        rows = in_ref[block * groups : (block + 1) * groups].reshape(groups * inner, columns)
+        at = slice(block * groups, (block + 1) * groups)
+        turned = [
+            in_ref[at, plane * row_group : (plane + 1) * row_group, :]
+            .reshape(groups * row_group, columns)
+            .T
+            for plane in range(inner // row_group)
+        ]
         table = y_block(tables, block, groups, parity)
-        term = triple(split(rows.T), split(table), ((1,), (0,)))
+        term = triple(split(jnp.concatenate(turned, 0)), split(table), ((1,), (0,)))
         total = term if total is None else total + term
     return total
 
@@ -276,9 +282,12 @@
 
 
 def middle_kernel(
-    has_extra, sections, in_ref, aux_ref, wx_ref, tw_cos, tw_sin, high_ref, low_ref, out_ref,
-    spec_ref, fil_ref, back_ref,
+    has_extra, sections, in_ref, aux_ref, wx_ref, tw_cos, tw_sin, ca, sa, cb, sb, *rest
 ):
+    if has_extra:
+        part_ref, out_ref, spec_ref, fil_ref, back_ref = rest
+    else:
+        out_ref, spec_ref, fil_ref, back_ref = rest
     devices, inner, columns = in_ref.shape
     kk = inner // 2
     slabs = devices // sections
@@ -324,7 +333,14 @@
                     spec_ref[j, 0, at, row : row + 8, :] = real
                     spec_ref[j, 1, at, row : row + 8, :] = imag
 
-    weights = (high_ref[...], low_ref[...])
+    cos_rows, sin_rows = [], []
+    cos_fine, sin_fine = cb[...], sb[...]
+    for group in range(ca.shape[0]):
+        cos_base, sin_base = ca[group : group + 1, :], sa[group : group + 1, :]
+        cos_rows.append(cos_base * cos_fine - sin_base * sin_fine)
+        sin_rows.append(sin_base * cos_fine + cos_base * sin_fine)
+    table = jnp.concatenate([jnp.concatenate(cos_rows, 0), jnp.concatenate(sin_rows, 0)], 1)
+    weights = split(table)
     total_zf = sections * zf_local
     for j in range(4):
         rows = spec_ref[j].reshape(2 * total_zf * padded, width)
@@ -393,9 +409,12 @@
                 for step in range(quarter):
                     target = section * slabs + a * quarter + step
                     piece = slice(step * lanes, (step + 1) * lanes)
-                    column = slice(plane * lanes, (plane + 1) * lanes)
-                    out_ref[target, row : row + 8, column] = real[:, piece]
-                    out_ref[target, kk + row : kk + row + 8, column] = imag[:, piece]
+                    at = plane * inner + row
+                    out_ref[target, at : at + 8, :] = real[:, piece]
+                    out_ref[target, at + kk : at + kk + 8, :] = imag[:, piece]
+    if has_extra:
+        for target in range(devices):
+            out_ref[target, planes * inner :, :] = part_ref[...]
 
 
 def kernel_call(body, out_shape, scratch, flops, moved, *operands):
@@ -430,10 +449,10 @@
     me = lax.axis_index("section") * slabs + lax.axis_index("slab")
     axes = ("section", "slab")
     base = np.arange(width)
-    turn = (base[:, None] * base[None, :] % width) * (2.0 * math.pi / width)
-    dft = np.concatenate([np.cos(turn), np.sin(turn)], 1).astype(np.float32)
-    dft_high = dft.astype(jnp.bfloat16)
-    dft_low = (dft - dft_high.astype(np.float32)).astype(jnp.bfloat16)
+    step = 2.0 * math.pi / width
+    coarse = base[::row_group, None] * base[None, :] % width * step
+    fine = base[:row_group, None] * base[None, :] % width * step
+    dft = [f(t).astype(np.float32) for t in (coarse, fine) for f in (np.cos, np.sin)]
     twist = np.arange(4)[:, None] * base[None, :] * (2.0 * math.pi / full_x)
     twist_cos, twist_sin = np.cos(twist).astype(np.float32), np.sin(twist).astype(np.float32)
     kx = np.arange(4)[:, None] + 4 * base[None, :]
@@ -442,6 +461,8 @@
     tables = [y_tables(full_y, devices, parity) for parity in range(2)]
     columns = planes * 2 * rows
     flops = 6 * half * half * columns
+    squared = concentration * concentration
+    bulk_sum = jnp.sum(0.25 * squared * squared - 0.5 * squared)
     arrived = []
     for parity in range(2):
         sent = kernel_call(
@@ -470,7 +491,7 @@
         aux = jnp.broadcast_to(aux[:, :, None], (3, padded, lanes))
         sent = kernel_call(
             functools.partial(middle_kernel, has_extra, sections),
-            (devices, 2 * kk, planes * rows),
+            (devices, 2 * kk * planes + (8 if has_extra else 0), rows),
             [
                 pltpu.VMEM((4, 2, 2 * full_z, padded, width), jnp.float32),
                 pltpu.VMEM((2, full_z, padded, width), jnp.float32),
@@ -483,8 +504,8 @@
             wave_x,
             twist_cos,
             twist_sin,
-            dft_high,
-            dft_low,
+            *dft,
+            *([jnp.full((8, lanes), bulk_sum)] if has_extra else []),
         )
         returned.append(lax.all_to_all(sent, axes, split_axis=0, concat_axis=0, tiled=True))
     even = kernel_call(
@@ -506,9 +527,7 @@
         even,
         *tables[1],
     )
-    squared = concentration * concentration
-    bulk_sum = jnp.sum(0.25 * squared * squared - 0.5 * squared)
-    energy = lax.psum(bulk_sum, axes) / cells
+    energy = jnp.sum(returned[0][:, 2 * kk * planes, 0]) / cells
     return (new_field, energy)
 
 

time: 210 us -> 189 us (0.900)
  blocking collectives: 45.1 us -> 0 us
  waiting for transfers between devices: 96.6 us -> 119 us
    psum x1 -> x0, blocking collectives: 45.1 us -> none  [kernel_step(): energy = lax.psum(bulk_sum, axes) / cells]
    all_to_all x4, waiting for transfers between devices: 96.6 us -> 119 us  [kernel_step(): lax.all_to_all(sent, axes, split_axis=0, concat_axis=0, tiled=True)]
  transfers between devices with their start and end apart: 4 -> 4, of which waited for: 3 -> 4; matrix products, arithmetic and copies ran while one was open for 1% -> 2% of each run, Pallas kernels for 16% -> 17%
where the time goes in v2:
time: 189 us; the launch traced here: 188 us
  waiting for transfers between devices  119 us (63%)
  Pallas kernels  44.3 us (23%)
  starting transfers between devices  16.6 us (9%)
  local copies, waits for them, and re-layouts  3.64 us (2%)
  between operations  2.51 us (1%)
    all_to_all x4, waiting for transfers between devices, kernel_step(): lax.all_to_all(sent, axes, split_axis=0, concat_axis=0, tiled=True)  119 us
    pallas_call x6, Pallas kernels, kernel_call(): pl.pallas_call(body, out_shape=jax.ShapeDtypeStruct(out_shape, jnp.float3...  44.3 us
    all_to_all x4, starting transfers between devices, kernel_step(): lax.all_to_all(sent, axes, split_axis=0, concat_axis=0, tiled=True)  16.6 us
  transfers between devices with their start and end apart: 4, of which 4 were waited for; matrix products, arithmetic and copies ran while one was open for 2% of the time, Pallas kernels for 17%

profile of v2, /device:TPU:0, one launch (start us, length us, event | category | flops | bytes accessed | tf_op | source)
XLA Modules:
  0.0 188.1 jit_solution(10721183070812238000)
XLA Ops:
  0.6 6.8 %shard_map.169 = f32[32,32,512]{2,1,0:T(8,128)} custom-call(f32[2,128,2048]{2,1,0:T(8,128)} %conc_ref.3, f32[32,1024]{1,0:T(8,128)} %constant.75.clone.ta, f32[32,1024]{1,0:T(8,128)} %constant.76.clone.tb, f32[32,1024]{1,0:T(8,128)} %constant.77.clone.tc, f32[32,1024]{1,0:T(8,128)} %constant.78.clone.td), custom_call_target="tpu_custom_call" | custom-call | flops 3221225472 | bytes 4194304 | tf_op jit(solution)/shard_map/pallas_call | solution.py:421
  7.5 7.5 %all-to-all-start.2 = ((f32[32,32,512]{2,1,0:T(8,128)}), f32[32,32,512]{2,1,0:T(8,128)}, u32[]{:S(2)}, u32[]{:S(2)}) async-start(f32[32,32,512]{2,1,0:T(8,128)} %shard_map.169), calls=%async_computation.2 | async-start | bytes 4194304 | tf_op jit(solution)/shard_map/all_to_all | solution.py:477
  14.9 6.8 %shard_map.167 = f32[32,32,512]{2,1,0:T(8,128)} custom-call(f32[2,128,2048]{2,1,0:T(8,128)} %conc_ref.3, f32[32,1024]{1,0:T(8,128)} %constant.79.clone.ta, f32[32,1024]{1,0:T(8,128)} %constant.80.clone.tb, f32[32,1024]{1,0:T(8,128)} %constant.77.clone.tc, f32[32,1024]{1,0:T(8,128)} %constant.78.clone.td), custom_call_target="tpu_custom_call" | custom-call | flops 3221225472 | bytes 4194304 | tf_op jit(solution)/shard_map/pallas_call | solution.py:421
  21.7 0.0 copy-start
  21.8 43.2 %all-to-all-done.2.in_ref = f32[32,32,512]{2,1,0:T(8,128)} async-done(((f32[32,32,512]{2,1,0:T(8,128)}), f32[32,32,512]{2,1,0:T(8,128)}, u32[]{:S(2)}, u32[]{:S(2)}) %all-to-all-start.2) | async-done | bytes 2097184 | tf_op jit(solution)/shard_map/all_to_all | solution.py:477
  65.0 3.7 %all-to-all-start = ((f32[32,32,512]{2,1,0:T(8,128)}), f32[32,32,512]{2,1,0:T(8,128)}, u32[]{:S(2)}, u32[]{:S(2)}) async-start(f32[32,32,512]{2,1,0:T(8,128)} %shard_map.167), calls=%async_computation | async-start | bytes 4194304 | tf_op jit(solution)/shard_map/all_to_all | solution.py:477
  68.7 0.0 copy-done
  68.7 1.1 fusion.1
  69.8 1.2 broadcast_in_dim.58.rest_0_
  71.1 0.7 broadcast_in_dim.57.aux_ref
  71.8 11.9 %shard_map.170 = f32[32,72,128]{2,1,0:T(8,128)} custom-call(f32[32,32,512]{2,1,0:T(8,128)} %all-to-all-done.2.in_ref, f32[3,24,128]{2,1,0:T(8,128)} %broadcast_in_dim.57.aux_ref, f32[4,512]{1,0:T(4,128)} %constant.81.clone.wx_ref, f32[4,512]{1,0:T(4,128)} %constant.82.clone.tw_cos, f32[4,512]{1,0:T(4,128)} %constant.83.clone.tw_sin, ...), custom_call_target="tpu_custom_call" | custom-call | flops 7247757312 | bytes 2097152 | tf_op jit(solution)/shard_map/pallas_call | solution.py:421
  83.6 34.9 %all-to-all-done.in_ref = f32[32,32,512]{2,1,0:T(8,128)} async-done(((f32[32,32,512]{2,1,0:T(8,128)}), f32[32,32,512]{2,1,0:T(8,128)}, u32[]{:S(2)}, u32[]{:S(2)}) %all-to-all-start) | async-done | bytes 2097184 | tf_op jit(solution)/shard_map/all_to_all | solution.py:477
  118.5 2.9 %all-to-all-start.3 = ((f32[32,72,128]{2,1,0:T(8,128)}), f32[32,72,128]{2,1,0:T(8,128)S(1)}, u32[]{:S(2)}, u32[]{:S(2)}) async-start(f32[32,72,128]{2,1,0:T(8,128)} %shard_map.170), calls=%async_computation.3 | async-start | bytes 2359296 | tf_op jit(solution)/shard_map/all_to_all | solution.py:510
  121.5 0.7 broadcast_in_dim.51.aux_ref
  122.2 9.4 %shard_map.168 = f32[32,64,128]{2,1,0:T(8,128)} custom-call(f32[32,32,512]{2,1,0:T(8,128)} %all-to-all-done.in_ref, f32[3,16,128]{2,1,0:T(8,128)} %broadcast_in_dim.51.aux_ref, f32[4,512]{1,0:T(4,128)} %constant.81.clone.wx_ref, f32[4,512]{1,0:T(4,128)} %constant.82.clone.tw_cos, f32[4,512]{1,0:T(4,128)} %constant.83.clone.tw_sin, ...), custom_call_target="tpu_custom_call" | custom-call | flops 4831838208 | bytes 2097152 | tf_op jit(solution)/shard_map/pallas_call | solution.py:421
  131.5 19.6 %all-to-all-done.3.in_ref = f32[32,72,128]{2,1,0:T(8,128)S(1)} async-done(((f32[32,72,128]{2,1,0:T(8,128)}), f32[32,72,128]{2,1,0:T(8,128)S(1)}, u32[]{:S(2)}, u32[]{:S(2)}) %all-to-all-start.3) | async-done | bytes 1179680 | tf_op jit(solution)/shard_map/all_to_all | solution.py:510
  151.2 0.0 copy-start.1
  151.2 2.6 %all-to-all-start.1 = ((f32[32,64,128]{2,1,0:T(8,128)}), f32[32,64,128]{2,1,0:T(8,128)S(1)}, u32[]{:S(2)}, u32[]{:S(2)}) async-start(f32[32,64,128]{2,1,0:T(8,128)} %shard_map.168), calls=%async_computation.1 | async-start | bytes 2097152 | tf_op jit(solution)/shard_map/all_to_all | solution.py:510
  153.8 0.6 slice_reduce_fusion
  155.1 0.0 copy-done.1
  155.1 4.4 %shard_map.171.even_ref = f32[256,1024]{1,0:T(8,128)} custom-call(f32[32,72,128]{2,1,0:T(8,128)} %copy-done.1, f32[32,1024]{1,0:T(8,128)} %constant.75.clone.ta, f32[32,1024]{1,0:T(8,128)} %constant.76.clone.tb, f32[32,1024]{1,0:T(8,128)} %constant.77.clone.tc, f32[32,1024]{1,0:T(8,128)} %constant.78.clone.td), custom_call_target="tpu_custom_call" | custom-call | flops 1610612736 | bytes 4194304 | tf_op jit(solution)/shard_map/pallas_call | solution.py:421
  159.5 21.5 %all-to-all-done.1.in_ref = f32[32,64,128]{2,1,0:T(8,128)S(1)} async-done(((f32[32,64,128]{2,1,0:T(8,128)}), f32[32,64,128]{2,1,0:T(8,128)S(1)}, u32[]{:S(2)}, u32[]{:S(2)}) %all-to-all-start.1) | async-done | bytes 1048608 | tf_op jit(solution)/shard_map/all_to_all | solution.py:510
  181.0 1.0 copy-done.2
  182.0 5.0 %shard_map.172 = f32[2,128,2048]{2,1,0:T(8,128)} custom-call(f32[32,64,128]{2,1,0:T(8,128)} %copy-done.2, f32[256,1024]{1,0:T(8,128)} %shard_map.171.even_ref, f32[32,1024]{1,0:T(8,128)} %constant.79.clone.ta, f32[32,1024]{1,0:T(8,128)} %constant.80.clone.tb, f32[32,1024]{1,0:T(8,128)} %constant.77.clone.tc, f32[32,1024]{1,0:T(8,128)} %constant.78.clone.td), custom_call_target="tpu_custom_call" | custom-call | flops 1610612736 | bytes 4194304 | tf_op jit(solution)/shard_map/pallas_call | solution.py:421
  (7 shorter events, 0.1 us)
Async XLA Ops:
  7.5 57.5 %all-to-all-start.2 = ((f32[32,32,512]{2,1,0:T(8,128)}), f32[32,32,512]{2,1,0:T(8,128)}, u32[]{:S(2)}, u32[]{:S(2)}) async-start(f32[32,32,512]{2,1,0:T(8,128)} %shard_map.169), calls=%async_computation.2 | async-start | bytes 4194304 | tf_op jit(solution)/shard_map/all_to_all | solution.py:477
  21.7 46.9 %copy-start = (f32[2,128,2048]{2,1,0:T(8,128)S(1)}, f32[2,128,2048]{2,1,0:T(8,128)}, u32[]{:S(2)}) copy-start(f32[2,128,2048]{2,1,0:T(8,128)} %conc_ref.3) | copy-start | bytes 6291460
  65.0 53.6 %all-to-all-start = ((f32[32,32,512]{2,1,0:T(8,128)}), f32[32,32,512]{2,1,0:T(8,128)}, u32[]{:S(2)}, u32[]{:S(2)}) async-start(f32[32,32,512]{2,1,0:T(8,128)} %shard_map.167), calls=%async_computation | async-start | bytes 4194304 | tf_op jit(solution)/shard_map/all_to_all | solution.py:477
  118.5 32.6 %all-to-all-start.3 = ((f32[32,72,128]{2,1,0:T(8,128)}), f32[32,72,128]{2,1,0:T(8,128)S(1)}, u32[]{:S(2)}, u32[]{:S(2)}) async-start(f32[32,72,128]{2,1,0:T(8,128)} %shard_map.170), calls=%async_computation.3 | async-start | bytes 2359296 | tf_op jit(solution)/shard_map/all_to_all | solution.py:510
  151.2 3.9 %copy-start.1 = (f32[32,72,128]{2,1,0:T(8,128)}, f32[32,72,128]{2,1,0:T(8,128)S(1)}, u32[]{:S(2)}) copy-start(f32[32,72,128]{2,1,0:T(8,128)S(1)} %all-to-all-done.3.in_ref) | copy-start | bytes 3538948
  151.2 29.8 %all-to-all-start.1 = ((f32[32,64,128]{2,1,0:T(8,128)}), f32[32,64,128]{2,1,0:T(8,128)S(1)}, u32[]{:S(2)}, u32[]{:S(2)}) async-start(f32[32,64,128]{2,1,0:T(8,128)} %shard_map.168), calls=%async_computation.1 | async-start | bytes 2097152 | tf_op jit(solution)/shard_map/all_to_all | solution.py:510
  181.0 1.0 copy-start.2
